TPU v7x, 512 devices: a 4x2x32 block of a 4x16x32 slice. The times are simulated.
512 devices in a mesh: groups: 2 (over y), row: 32 (over z), col: 4 (over x), sub: 2 (over core).
Axes of the slice: x: 4, y: 2, z: 32, core: 2. Of those that a mesh axis runs over, the one named last changes fastest.
The devices are a block of a 4x16x32 slice.
Arguments:
- matrix: float32 [16384, 8192], P(('groups', 'row'), ('col', 'sub')), parts along dimension 0, may hold values from -60 to 60
- basis_vectors: float32 [16384, 1024], P(('groups', 'row'), ('col', 'sub')), parts along dimension 0, may hold values from -0.0625 to 0.0625
- split_size: int32 [2], P('groups'), parts along dimension 0, may hold values from 256 to 767
Outputs:
- children: float32 [2, 2048, 1024], P('sub', ('groups', 'row'), 'col'), parts along dimension 1
There are 2 independent parts, one for each index of `groups`. A program takes and returns all parts, laid end to end along the dimension named above; each array names one. Nothing has to cross between parts.
Inputs may be any that keep to these rules, and one draw needn't show every extreme that they name: The second subspace has 1024 minus split_size vectors.
All inputs are finite; a program needn't handle non-finite values.
Results may differ from a plain program's by a relative error of at most 0.00011.
Values sent between devices are 32-bit elements; how exact they have to be, the bound alone decides.
No kernel may reach another device: no remote copies, remote signals or barrier semaphores. Data moves between devices by JAX's collectives and lax.ppermute only.
A program may use at most 64 MiB of HBM per device.

v0:
```python
import jax
import jax.numpy as jnp
from jax import lax
from jax.sharding import PartitionSpec as P


def cut_along(array, dim, size):
    before, after = (array.shape[:dim], array.shape[dim + 1 :])
    return jnp.moveaxis(array.reshape(*before, size, -1, *after), dim, 0)


def sent_and_summed(array, axis, dim):
    size = lax.axis_size(axis)
    pieces = lax.all_to_all(cut_along(array, dim, size), axis, 0, 0, tiled=True)
    return jnp.sum(pieces, axis=0)


def copy_for_each(array, axis):
    size = lax.axis_size(axis)
    return lax.all_to_all(
        jnp.broadcast_to(array[None], (size, *array.shape)), axis, 0, 0, tiled=True
    )


def laid_out(pieces, dim):
    dims = list(pieces.shape[1:])
    dims[dim] *= pieces.shape[0]
    return jnp.moveaxis(pieces, 0, dim).reshape(dims)


def gathered_copies(array, axis, dim):
    pieces = copy_for_each(array, axis)
    return laid_out(pieces, dim)


def shards(matrix, basis_vectors, split_size):
    strip = lax.all_gather(basis_vectors, "row", axis=0, tiled=True)
    row_panel = lax.all_to_all(strip, ("col", "sub"), split_axis=0, concat_axis=1, tiled=True)
    partial_image = jnp.dot(
        matrix, row_panel, precision=lax.Precision.HIGHEST, preferred_element_type=jnp.float32
    )
    image = sent_and_summed(partial_image, ("col", "sub"), 1)
    partial_proj = lax.dot_general(
        gathered_copies(basis_vectors, ("col", "sub"), 1),
        image,
        (((0,), (0,)), ((), ())),
        precision=lax.Precision.HIGHEST,
        preferred_element_type=jnp.float32,
    )
    proj_block = sent_and_summed(partial_proj, "row", 0)
    child_block = lax.all_gather(proj_block, "sub", axis=1, tiled=True)
    row_ids = (
        jnp.arange(child_block.shape[0], dtype=jnp.int32)
        + lax.axis_index("row") * child_block.shape[0]
    )
    col_ids = (
        jnp.arange(child_block.shape[1], dtype=jnp.int32)
        + lax.axis_index("col") * child_block.shape[1]
    )
    leading = split_size[0]
    row_first = row_ids < leading
    col_first = col_ids < leading
    mask_one = row_first[:, None] & col_first[None, :]
    mask_two = jnp.logical_not(row_first)[:, None] & jnp.logical_not(col_first)[None, :]
    selected = jnp.where(lax.axis_index("sub") == 0, mask_one, mask_two)
    return jnp.where(selected, child_block, jnp.zeros((), jnp.float32))[None]


def solution(mesh):
    placed = (
        P(("groups", "row"), ("col", "sub")),
        P(("groups", "row"), ("col", "sub")),
        P("groups"),
    )
    return jax.shard_map(
        shards,
        mesh=mesh,
        in_specs=placed,
        out_specs=P("sub", ("groups", "row"), "col"),
        check_vma=False,
    )
```

profile of v0, /device:TPU:33, one launch (start us, length us, event | category | flops | bytes accessed | tf_op | source)
XLA Modules:
  0.0 370.7 jit_solution(7150744775797212419)
XLA Ops:
  6.5 0.0 copy-start
  6.6 0.0 all-gather.2.cloned.1.call-start
  6.6 0.7 all-gather.2.cloned.1.call-update
  7.3 148.1 %all-gather.2.cloned.1.call-done = f32[8192,128]{1,0:T(8,128)} async-done(((f32[256,128]{1,0:T(8,128)}), f32[8192,128]{1,0:T(8,128)}) %all-gather.2.cloned.1.call-update) | async-done | bytes 4194320 | tf_op jit(solution)/shard_map/all_gather | solution.py:37
  155.4 74.3 %all_to_all.34 = f32[8,1024,128]{2,1,0:T(8,128)} all-to-all(f32[8,1024,128]{2,1,0:T(8,128)} %bitcast.30), channel_id=1, replica_groups=mesh['groups'=2,'row'=32,'col'=4,'sub'=2] {'col','sub'}, dimensions={0} | all-to-all | bytes 8388608 | tf_op jit(solution)/shard_map/all_to_all | solution.py:38
  229.7 5.4 %copy.6 = f32[1024,8,128]{0,2,1:T(8,128)} copy(f32[1024,8,128]{2,0,1:T(8,128)} %bitcast.29) | data formatting | bytes 8388608 | tf_op jit(solution)/shard_map/all_to_all | solution.py:38
  235.1 0.0 copy-done
  235.1 0.0 copy-start.1
  235.1 6.3 %fusion.2 = f32[8,256,128]{2,1,0:T(8,128)} fusion(f32[1024,8,128]{0,2,1:T(8,128)} %copy.6, f32[256,1024]{1,0:T(8,128)S(1)} %copy-done), kind=kOutput, calls=%fused_computation.2 | convolution fusion | flops 3221225472 | bytes 6291456 | tf_op jit(solution)/shard_map/dot_general | solution.py:39
  241.4 4.5 %all-to-all-start.1 = ((f32[8,256,128]{2,1,0:T(8,128)}), f32[8,256,128]{2,1,0:T(8,128)S(1)}, u32[]{:S(2)}, u32[]{:S(2)}) async-start(f32[8,256,128]{2,1,0:T(8,128)} %fusion.2), calls=%async_computation.1 | async-start | bytes 2097152 | tf_op jit(solution)/shard_map/all_to_all | solution.py:14
  245.9 0.0 copy-done.1
  245.9 0.1 copy.7
  246.0 15.0 %all-to-all-done.1 = f32[8,256,128]{2,1,0:T(8,128)S(1)} async-done(((f32[8,256,128]{2,1,0:T(8,128)}), f32[8,256,128]{2,1,0:T(8,128)S(1)}, u32[]{:S(2)}, u32[]{:S(2)}) %all-to-all-start.1) | async-done | bytes 1048608 | tf_op jit(solution)/shard_map/all_to_all | solution.py:14
  261.0 1.1 broadcast_in_dim.7
  262.0 4.4 %all-to-all-start.2 = ((f32[8,256,128]{1,2,0:T(8,128)}), f32[8,256,128]{1,2,0:T(8,128)S(1)}, u32[]{:S(2)}, u32[]{:S(2)}) async-start(f32[8,256,128]{1,2,0:T(8,128)} %broadcast_in_dim.7), calls=%async_computation.2 | async-start | bytes 2097152 | tf_op jit(solution)/shard_map/all_to_all | solution.py:20
  266.4 0.1 reduce_sum.18
  266.5 15.0 %all-to-all-done.2 = f32[8,256,128]{1,2,0:T(8,128)S(1)} async-done(((f32[8,256,128]{1,2,0:T(8,128)}), f32[8,256,128]{1,2,0:T(8,128)S(1)}, u32[]{:S(2)}, u32[]{:S(2)}) %all-to-all-start.2) | async-done | bytes 1048608 | tf_op jit(solution)/shard_map/all_to_all | solution.py:20
  281.5 1.2 convolution_bitcast_fusion
  282.7 1.0 copy.8
  283.7 12.6 %all-to-all-start.3 = ((f32[32,32,128]{2,1,0:T(8,128)}), f32[32,32,128]{2,1,0:T(8,128)S(1)}, u32[]{:S(2)}, u32[]{:S(2)}) async-start(f32[32,32,128]{2,1,0:T(8,128)} %bitcast.11), calls=%async_computation.3 | async-start | bytes 1048576 | tf_op jit(solution)/shard_map/all_to_all | solution.py:14
  297.0 63.0 %all-to-all-done.3 = f32[32,32,128]{2,1,0:T(8,128)S(1)} async-done(((f32[32,32,128]{2,1,0:T(8,128)}), f32[32,32,128]{2,1,0:T(8,128)S(1)}, u32[]{:S(2)}, u32[]{:S(2)}) %all-to-all-start.3) | async-done | bytes 524320 | tf_op jit(solution)/shard_map/all_to_all | solution.py:14
  360.1 3.1 all_gather.7
  363.2 0.7 select_bitcast_fusion
  (3 shorter events, 0.1 us)
Async XLA Ops:
  6.5 228.5 %copy-start = (f32[256,1024]{1,0:T(8,128)S(1)}, f32[256,1024]{1,0:T(8,128)}, u32[]{:S(2)}) copy-start(f32[256,1024]{1,0:T(8,128)} %param.3) | copy-start | bytes 3145732
  6.6 148.8 %all-gather.2.cloned.1.call-start = ((), (), s32[]{:S(2)}) async-start(), calls=%async_computation.4 | async-start | bytes 4325376 | tf_op jit(solution)/shard_map/all_gather | solution.py:37
  235.1 10.8 %copy-start.1 = (f32[256,128]{1,0:T(8,128)S(1)}, f32[256,128]{1,0:T(8,128)}, u32[]{:S(2)}) copy-start(f32[256,128]{1,0:T(8,128)} %param.4) | copy-start | bytes 393220
  241.4 19.6 %all-to-all-start.1 = ((f32[8,256,128]{2,1,0:T(8,128)}), f32[8,256,128]{2,1,0:T(8,128)S(1)}, u32[]{:S(2)}, u32[]{:S(2)}) async-start(f32[8,256,128]{2,1,0:T(8,128)} %fusion.2), calls=%async_computation.1 | async-start | bytes 2097152 | tf_op jit(solution)/shard_map/all_to_all | solution.py:14
  262.0 19.5 %all-to-all-start.2 = ((f32[8,256,128]{1,2,0:T(8,128)}), f32[8,256,128]{1,2,0:T(8,128)S(1)}, u32[]{:S(2)}, u32[]{:S(2)}) async-start(f32[8,256,128]{1,2,0:T(8,128)} %broadcast_in_dim.7), calls=%async_computation.2 | async-start | bytes 2097152 | tf_op jit(solution)/shard_map/all_to_all | solution.py:20
  283.7 76.3 %all-to-all-start.3 = ((f32[32,32,128]{2,1,0:T(8,128)}), f32[32,32,128]{2,1,0:T(8,128)S(1)}, u32[]{:S(2)}, u32[]{:S(2)}) async-start(f32[32,32,128]{2,1,0:T(8,128)} %bitcast.11), calls=%async_computation.3 | async-start | bytes 1048576 | tf_op jit(solution)/shard_map/all_to_all | solution.py:14
Sparse Core Ops, SparseCore 0:
  9.4 145.8 all-gather.1
where the time goes:
time: 371 us
  waiting for transfers between devices  242 us (65%)
  blocking collectives  77.4 us (21%)
  starting transfers between devices  21.5 us (6%)
  between operations  14.1 us (4%)
  matrix products  7.56 us (2%)
  local copies, waits for them, and re-layouts  7.52 us (2%)
    all_gather x1, waiting for transfers between devices, shards(): strip = lax.all_gather(basis_vectors, 'row', axis=0, tiled=True)  148 us
    all_to_all x2, waiting for transfers between devices, sent_and_summed(): pieces = lax.all_to_all(cut_along(array, dim, size), axis, 0, 0, tiled=True)  78 us
    all_to_all x1, blocking collectives, shards(): lax.all_to_all(strip, ('col', 'sub'), split_axis=0, concat_axis=1, tiled=...  74.3 us
    all_to_all x2, starting transfers between devices, sent_and_summed(): pieces = lax.all_to_all(cut_along(array, dim, size), axis, 0, 0, tiled=True)  17.1 us
    all_to_all x1, waiting for transfers between devices, copy_for_each(): lax.all_to_all(jnp.broadcast_to(array[None], (size, *array.shape)), axis,...  15 us
  transfers between devices with their start and end apart: 4, of which 4 were waited for; matrix products, arithmetic and copies ran while one was open for 0% of the time, Pallas kernels for 0%

commit v1 on v0

--- a/solution.py
+++ b/solution.py
@@ -34,7 +34,10 @@
 
 
 def shards(matrix, basis_vectors, split_size):
-    strip = lax.all_gather(basis_vectors, "row", axis=0, tiled=True)
+    count = lax.axis_size("row")
+    blocks = jnp.stack([basis_vectors for _ in range(count)])
+    blocks = lax.all_to_all(blocks, "row", split_axis=0, concat_axis=0)
+    strip = jnp.concatenate(blocks, axis=0)
     row_panel = lax.all_to_all(strip, ("col", "sub"), split_axis=0, concat_axis=1, tiled=True)
     partial_image = jnp.dot(
         matrix, row_panel, precision=lax.Precision.HIGHEST, preferred_element_type=jnp.float32

time: 371 us -> 606 us (1.63)
  blocking collectives: 77.4 us -> 477 us
  waiting for transfers between devices: 242 us -> 93 us
  between operations: 14.1 us -> 0.71 us
    all_to_all x0 -> x1, blocking collectives: none -> 420 us  [shards(): blocks = lax.all_to_all(blocks, 'row', split_axis=0, concat_axis=0)]
    all_gather x1 -> x0, waiting for transfers between devices: 148 us -> none  [shards(): strip = lax.all_gather(basis_vectors, 'row', axis=0, tiled=True)]
    all_to_all x1, blocking collectives: 74.3 us -> 54 us  [shards(): lax.all_to_all(strip, ('col', 'sub'), split_axis=0, concat_axis=1, tiled=...]
  transfers between devices with their start and end apart: 4 -> 3, of which waited for: 4 -> 3; matrix products, arithmetic and copies ran while one was open for 0% -> 0% of each run, Pallas kernels for 0% -> 0%
where the time goes in v1:
time: 606 us; the launch traced here: 605 us
  blocking collectives  477 us (79%)
  waiting for transfers between devices  93 us (15%)
  starting transfers between devices  16.8 us (3%)
  local copies, waits for them, and re-layouts  8.96 us (1%)
  matrix products  7.58 us (1%)
    all_to_all x1, blocking collectives, shards(): blocks = lax.all_to_all(blocks, 'row', split_axis=0, concat_axis=0)  420 us
    all_to_all x2, waiting for transfers between devices, sent_and_summed(): pieces = lax.all_to_all(cut_along(array, dim, size), axis, 0, 0, tiled=True)  78 us
    all_to_all x1, blocking collectives, shards(): lax.all_to_all(strip, ('col', 'sub'), split_axis=0, concat_axis=1, tiled=...  54 us
    all_to_all x1, waiting for transfers between devices, copy_for_each(): lax.all_to_all(jnp.broadcast_to(array[None], (size, *array.shape)), axis,...  15 us
    all_to_all x2, starting transfers between devices, sent_and_summed(): pieces = lax.all_to_all(cut_along(array, dim, size), axis, 0, 0, tiled=True)  12.4 us
  transfers between devices with their start and end apart: 3, of which 3 were waited for; matrix products, arithmetic and copies ran while one was open for 0% of the time, Pallas kernels for 0%

profile of v1, /device:TPU:33, one launch (start us, length us, event | category | flops | bytes accessed | tf_op | source)
XLA Modules:
  0.0 605.2 jit_solution(3029789306048276531)
XLA Ops:
  0.0 0.0 copy-start
  0.0 1.5 stack.2
  1.5 420.2 %all_to_all.39 = f32[32,256,128]{2,1,0:T(8,128)S(1)} all-to-all(f32[32,256,128]{2,1,0:T(8,128)S(1)} %stack.2), channel_id=1, replica_groups=mesh['groups'=2,'row'=32,'col'=4,'sub'=2] {'row'}, dimensions={0} | all-to-all | bytes 8388608 | tf_op jit(solution)/shard_map/all_to_all | solution.py:39
  421.7 54.0 %all_to_all.40 = f32[8,1024,128]{2,1,0:T(8,128)} all-to-all(f32[8,1024,128]{2,1,0:T(8,128)S(1)} %bitcast.29), channel_id=1, replica_groups=mesh['groups'=2,'row'=32,'col'=4,'sub'=2] {'col','sub'}, dimensions={0} | all-to-all | bytes 8388608 | tf_op jit(solution)/shard_map/all_to_all | solution.py:41
  475.7 5.3 copy.6
  481.0 0.0 copy-done
  481.0 0.0 copy-start.1
  481.0 6.3 %fusion.2 = f32[8,256,128]{2,1,0:T(8,128)} fusion(f32[1024,8,128]{0,2,1:T(8,128)} %copy.6, f32[256,1024]{1,0:T(8,128)S(1)} %copy-done), kind=kOutput, calls=%fused_computation.2 | convolution fusion | flops 3221225472 | bytes 6291456 | tf_op jit(solution)/shard_map/dot_general | solution.py:42
  487.4 4.5 all-to-all-start.2
  491.9 0.0 copy-done.1
  491.9 0.1 copy.7
  492.0 15.0 %all-to-all-done.2 = f32[8,256,128]{2,1,0:T(8,128)S(1)} async-done(((f32[8,256,128]{2,1,0:T(8,128)}), f32[8,256,128]{2,1,0:T(8,128)S(1)}, u32[]{:S(2)}, u32[]{:S(2)}) %all-to-all-start.2) | async-done | bytes 1048608 | tf_op jit(solution)/shard_map/all_to_all | solution.py:14
  507.0 1.1 broadcast_in_dim.7
  508.0 4.4 all-to-all-start.3
  512.4 0.1 reduce_sum.18
  512.5 15.0 %all-to-all-done.3 = f32[8,256,128]{1,2,0:T(8,128)S(1)} async-done(((f32[8,256,128]{1,2,0:T(8,128)}), f32[8,256,128]{1,2,0:T(8,128)S(1)}, u32[]{:S(2)}, u32[]{:S(2)}) %all-to-all-start.3) | async-done | bytes 1048608 | tf_op jit(solution)/shard_map/all_to_all | solution.py:20
  527.5 1.2 convolution_bitcast_fusion
  528.7 1.0 copy.8
  529.7 7.8 %all-to-all-start.4 = ((f32[32,32,128]{2,1,0:T(8,128)}), f32[32,32,128]{2,1,0:T(8,128)S(1)}, u32[]{:S(2)}, u32[]{:S(2)}) async-start(f32[32,32,128]{2,1,0:T(8,128)} %bitcast.11), calls=%async_computation.4 | async-start | bytes 1048576 | tf_op jit(solution)/shard_map/all_to_all | solution.py:14
  538.3 63.0 %all-to-all-done.4 = f32[32,32,128]{2,1,0:T(8,128)S(1)} async-done(((f32[32,32,128]{2,1,0:T(8,128)}), f32[32,32,128]{2,1,0:T(8,128)S(1)}, u32[]{:S(2)}, u32[]{:S(2)}) %all-to-all-start.4) | async-done | bytes 524320 | tf_op jit(solution)/shard_map/all_to_all | solution.py:14
  601.4 3.1 all_gather.3
  604.5 0.7 select_bitcast_fusion
  (3 shorter events, 0.1 us)
Async XLA Ops:
  0.0 481.0 %copy-start = (f32[256,1024]{1,0:T(8,128)S(1)}, f32[256,1024]{1,0:T(8,128)}, u32[]{:S(2)}) copy-start(f32[256,1024]{1,0:T(8,128)} %param.3) | copy-start | bytes 3145732
  481.0 10.9 %copy-start.1 = (f32[256,128]{1,0:T(8,128)S(1)}, f32[256,128]{1,0:T(8,128)}, u32[]{:S(2)}) copy-start(f32[256,128]{1,0:T(8,128)} %param.4) | copy-start | bytes 393220
  487.4 19.6 %all-to-all-start.2 = ((f32[8,256,128]{2,1,0:T(8,128)}), f32[8,256,128]{2,1,0:T(8,128)S(1)}, u32[]{:S(2)}, u32[]{:S(2)}) async-start(f32[8,256,128]{2,1,0:T(8,128)} %fusion.2), calls=%async_computation.2 | async-start | bytes 2097152 | tf_op jit(solution)/shard_map/all_to_all | solution.py:14
  508.0 19.5 %all-to-all-start.3 = ((f32[8,256,128]{1,2,0:T(8,128)}), f32[8,256,128]{1,2,0:T(8,128)S(1)}, u32[]{:S(2)}, u32[]{:S(2)}) async-start(f32[8,256,128]{1,2,0:T(8,128)} %broadcast_in_dim.7), calls=%async_computation.3 | async-start | bytes 2097152 | tf_op jit(solution)/shard_map/all_to_all | solution.py:20
  529.7 71.6 %all-to-all-start.4 = ((f32[32,32,128]{2,1,0:T(8,128)}), f32[32,32,128]{2,1,0:T(8,128)S(1)}, u32[]{:S(2)}, u32[]{:S(2)}) async-start(f32[32,32,128]{2,1,0:T(8,128)} %bitcast.11), calls=%async_computation.4 | async-start | bytes 1048576 | tf_op jit(solution)/shard_map/all_to_all | solution.py:14

commit v2 on v0

--- a/solution.py
+++ b/solution.py
@@ -2,6 +2,12 @@
 import jax.numpy as jnp
 from jax import lax
 from jax.sharding import PartitionSpec as P
+
+
+def stacked_exchange(block, name, split, join):
+    pieces = jnp.split(block, lax.axis_size(name), axis=split)
+    received = lax.all_to_all(jnp.stack(pieces), name, 0, 0)
+    return jnp.concatenate(received, axis=join)
 
 
 def cut_along(array, dim, size):
@@ -35,7 +41,7 @@
 
 def shards(matrix, basis_vectors, split_size):
     strip = lax.all_gather(basis_vectors, "row", axis=0, tiled=True)
-    row_panel = lax.all_to_all(strip, ("col", "sub"), split_axis=0, concat_axis=1, tiled=True)
+    row_panel = stacked_exchange(strip, ("col", "sub"), 0, 1)
     partial_image = jnp.dot(
         matrix, row_panel, precision=lax.Precision.HIGHEST, preferred_element_type=jnp.float32
     )

time: 371 us -> 371 us (level)
  blocking collectives: 77.4 us -> 95.4 us
  waiting for transfers between devices: 242 us -> 225 us
  local copies, waits for them, and re-layouts: 7.52 us -> 12.4 us
  starting transfers between devices: 21.5 us -> 17.1 us
    all_to_all x1 -> x2, blocking collectives: 74.3 us -> 92.3 us  [the longest x1 73.8 us: stacked_exchange(): received = lax.all_to_all(jnp.stack(pieces), name, 0, 0)]
    all_to_all x2 -> x1, waiting for transfers between devices: 78 us -> 63 us  [sent_and_summed(): pieces = lax.all_to_all(cut_along(array, dim, size), axis, 0, 0, tiled=True)]
    unnamed x5 -> x12, local copies, waits for them, and re-layouts: 0.1 us -> 9.28 us
    all_to_all x1 -> x0, local copies, waits for them, and re-layouts: 5.37 us -> none  [shards(): lax.all_to_all(strip, ('col', 'sub'), split_axis=0, concat_axis=1, tiled=...]
    all_to_all x2 -> x1, starting transfers between devices: 17.1 us -> 12.6 us  [sent_and_summed(): pieces = lax.all_to_all(cut_along(array, dim, size), axis, 0, 0, tiled=True)]
  transfers between devices with their start and end apart: 4 -> 3, of which waited for: 4 -> 3; matrix products, arithmetic and copies ran while one was open for 0% -> 0% of each run, Pallas kernels for 0% -> 0%
where the time goes in v2:
time: 371 us; the launch traced here: 370 us
  waiting for transfers between devices  225 us (61%)
  blocking collectives  95.4 us (26%)
  starting transfers between devices  17.1 us (5%)
  between operations  14.2 us (4%)
  local copies, waits for them, and re-layouts  12.4 us (3%)
  matrix products  4.67 us (1%)
    all_gather x1, waiting for transfers between devices, shards(): strip = lax.all_gather(basis_vectors, 'row', axis=0, tiled=True)  147 us
    all_to_all x1, blocking collectives, stacked_exchange(): received = lax.all_to_all(jnp.stack(pieces), name, 0, 0)  73.8 us
    all_to_all x1, waiting for transfers between devices, sent_and_summed(): pieces = lax.all_to_all(cut_along(array, dim, size), axis, 0, 0, tiled=True)  63 us
    all_to_all x1, blocking collectives, sent_and_summed(): pieces = lax.all_to_all(cut_along(array, dim, size), axis, 0, 0, tiled=True)  18.5 us
    all_to_all x1, waiting for transfers between devices, copy_for_each(): lax.all_to_all(jnp.broadcast_to(array[None], (size, *array.shape)), axis,...  15 us
    all_to_all x1, starting transfers between devices, sent_and_summed(): pieces = lax.all_to_all(cut_along(array, dim, size), axis, 0, 0, tiled=True)  12.6 us
    unnamed x12, local copies, waits for them, and re-layouts  9.28 us
  transfers between devices with their start and end apart: 3, of which 3 were waited for; matrix products, arithmetic and copies ran while one was open for 0% of the time, Pallas kernels for 0%

profile of v2, /device:TPU:33, one launch (start us, length us, event | category | flops | bytes accessed | tf_op | source)
XLA Modules:
  0.0 369.8 jit_solution(2510449901732508686)
XLA Ops:
  6.5 0.0 copy-start
  6.6 0.0 all-gather.2.cloned.1.call-start
  6.6 1.7 copy.7
  8.3 0.1 all-gather.2.cloned.1.call-update
  8.3 147.1 %all-gather.2.cloned.1.call-done = f32[8192,128]{0,1:T(8,128)} async-done(((f32[256,128]{0,1:T(8,128)}), f32[8192,128]{0,1:T(8,128)}) %all-gather.2.cloned.1.call-update) | async-done | bytes 4194320 | tf_op jit(solution)/shard_map/all_gather | solution.py:43
  155.5 1.1 fusion.7
  156.5 1.1 fusion.6
  157.6 1.1 fusion.5
  158.7 1.1 fusion.4
  159.8 1.1 fusion.3
  160.9 1.1 fusion.2
  162.0 1.1 fusion.1
  163.0 1.1 fusion
  164.1 73.8 %all_to_all.20 = f32[8,1024,128]{1,2,0:T(8,128)S(1)} all-to-all(f32[8,1024,128]{1,2,0:T(8,128)S(1)} %fusion), channel_id=1, replica_groups=mesh['groups'=2,'row'=32,'col'=4,'sub'=2] {'col','sub'}, dimensions={0} | all-to-all | bytes 8388608 | tf_op jit(solution)/shard_map/all_to_all | solution.py:9
  238.0 0.0 copy-done
  238.0 0.0 copy-start.1
  238.0 3.5 fusion.10
  241.4 18.5 %all_to_all.21 = f32[8,256,128]{1,2,0:T(8,128)S(1)} all-to-all(f32[8,256,128]{1,2,0:T(8,128)S(1)} %bitcast.57), channel_id=1, replica_groups=mesh['groups'=2,'row'=32,'col'=4,'sub'=2] {'col','sub'}, dimensions={0} | all-to-all | bytes 2097152 | tf_op jit(solution)/shard_map/all_to_all | solution.py:20
  259.9 0.0 copy-done.1
  259.9 1.1 broadcast_in_dim.7
  261.0 4.5 %all-to-all-start.2 = ((f32[8,256,128]{1,2,0:T(8,128)}), f32[8,256,128]{1,2,0:T(8,128)S(1)}, u32[]{:S(2)}, u32[]{:S(2)}) async-start(f32[8,256,128]{1,2,0:T(8,128)} %broadcast_in_dim.7), calls=%async_computation.2 | async-start | bytes 2097152 | tf_op jit(solution)/shard_map/all_to_all | solution.py:26
  265.5 0.1 reduce_sum.18
  265.6 15.0 %all-to-all-done.2 = f32[8,256,128]{1,2,0:T(8,128)S(1)} async-done(((f32[8,256,128]{1,2,0:T(8,128)}), f32[8,256,128]{1,2,0:T(8,128)S(1)}, u32[]{:S(2)}, u32[]{:S(2)}) %all-to-all-start.2) | async-done | bytes 1048608 | tf_op jit(solution)/shard_map/all_to_all | solution.py:26
  280.6 1.2 convolution_bitcast_fusion
  281.8 1.0 copy.9
  282.8 12.6 %all-to-all-start.3 = ((f32[32,32,128]{2,1,0:T(8,128)}), f32[32,32,128]{2,1,0:T(8,128)S(1)}, u32[]{:S(2)}, u32[]{:S(2)}) async-start(f32[32,32,128]{2,1,0:T(8,128)} %bitcast.17), calls=%async_computation.3 | async-start | bytes 1048576 | tf_op jit(solution)/shard_map/all_to_all | solution.py:20
  296.1 63.0 %all-to-all-done.3 = f32[32,32,128]{2,1,0:T(8,128)S(1)} async-done(((f32[32,32,128]{2,1,0:T(8,128)}), f32[32,32,128]{2,1,0:T(8,128)S(1)}, u32[]{:S(2)}, u32[]{:S(2)}) %all-to-all-start.3) | async-done | bytes 524320 | tf_op jit(solution)/shard_map/all_to_all | solution.py:20
  359.2 3.1 all_gather.7
  362.3 0.7 select_bitcast_fusion
  (3 shorter events, 0.1 us)
Async XLA Ops:
  6.5 231.4 %copy-start = (f32[256,1024]{1,0:T(8,128)S(1)}, f32[256,1024]{1,0:T(8,128)}, u32[]{:S(2)}) copy-start(f32[256,1024]{1,0:T(8,128)} %param.3) | copy-start | bytes 3145732
  6.6 148.9 %all-gather.2.cloned.1.call-start = ((), (), s32[]{:S(2)}) async-start(), calls=%async_computation.4 | async-start | bytes 4325376 | tf_op jit(solution)/shard_map/all_gather | solution.py:43
  238.0 22.0 %copy-start.1 = (f32[256,128]{0,1:T(8,128)S(1)}, f32[256,128]{0,1:T(8,128)}, u32[]{:S(2)}) copy-start(f32[256,128]{0,1:T(8,128)} %copy.7) | copy-start | bytes 393220
  261.0 19.6 %all-to-all-start.2 = ((f32[8,256,128]{1,2,0:T(8,128)}), f32[8,256,128]{1,2,0:T(8,128)S(1)}, u32[]{:S(2)}, u32[]{:S(2)}) async-start(f32[8,256,128]{1,2,0:T(8,128)} %broadcast_in_dim.7), calls=%async_computation.2 | async-start | bytes 2097152 | tf_op jit(solution)/shard_map/all_to_all | solution.py:26
  282.8 76.4 %all-to-all-start.3 = ((f32[32,32,128]{2,1,0:T(8,128)}), f32[32,32,128]{2,1,0:T(8,128)S(1)}, u32[]{:S(2)}, u32[]{:S(2)}) async-start(f32[32,32,128]{2,1,0:T(8,128)} %bitcast.17), calls=%async_computation.3 | async-start | bytes 1048576 | tf_op jit(solution)/shard_map/all_to_all | solution.py:20
Sparse Core Ops, SparseCore 0:
  9.4 145.9 all-gather.1
